TPU v7x, 32 devices: a whole 2x2x4 slice. The times are simulated.
32 devices in a mesh: pts: 16 (over z, y, core), cen: 2 (over x).
Axes of the slice: x: 2, y: 2, z: 4, core: 2. Of those that a mesh axis runs over, the one named last changes fastest.
Arguments:
- points: bfloat16 [4096, 256], P('pts'), may hold values from -64 to 64
- centroids: bfloat16 [65536, 256], P('cen'), may hold values from -10 to 10
Outputs:
- updated: float32 [65536, 256], P(('cen', 'pts'))
- log_norm: float32 [4096], P('pts')
All inputs are finite; a program needn't handle non-finite values.
Results may differ from a plain program's by a relative error of at most 0.0017.
Values may be sent and summed in bfloat16 or wider, within the bound.
A program may use at most 128 MiB of HBM per device.

v0:
```python
import functools
import math

import jax
import jax.numpy as jnp
from jax import lax
from jax.experimental import pallas as pl
from jax.experimental.pallas import tpu as pltpu
from jax.sharding import PartitionSpec as P

inv_temp = 0.0625
prior_count = 1.0
log2e = math.log2(math.e)
MESH = pl.DeviceIdType.MESH


def kernel(
    G, C, points_ref, table_ref, out_ref, norm_ref,
    pts_all, pts_scaled, table, half_norms, scores, shares,
    peaks, local_log, all_local, every_norm, factors,
    load_sem, send_sem, ring_sem, twin_sem, stat_send, stat_recv, norm_send, norm_recv,
):
    T, D = points_ref.shape
    own = table.shape[0]
    R = G // 2
    far = R // 2
    half = T // 2
    N = G * C
    RB = min(256, own)
    NB = own // RB
    me = lax.axis_index("pts")
    cen = lax.axis_index("cen")
    mine = cen * G + me
    core = me % 2
    chip = me // 2
    turn = chip % 2
    pos = (chip // 2) * (1 - turn) + (R - 1 - chip // 2) * turn

    def tile_at(p, c):
        s = p // far
        return ((1 - s) * 2 * p + s * (2 * (R - 1 - p) + 1)) * 2 + c

    twin = me + 1 - 2 * core
    right = tile_at((pos + 1) % R, core)
    left = tile_at((pos + R - 1) % R, core)

    my_points = pts_all.at[pl.ds(pl.multiple_of(me * T, T), T)]
    load_points = pltpu.make_async_copy(points_ref, my_points, load_sem.at[0])
    load_points.start()
    load_table = pltpu.make_async_copy(
        table_ref.at[pl.ds(pl.multiple_of(me * own, own), own)], table, load_sem.at[1]
    )
    load_table.start()

    barrier = pltpu.get_barrier_semaphore()

    for peer in (right, left, twin):
        pl.semaphore_signal(
            barrier, inc=1, device_id={"pts": peer, "cen": cen}, device_id_type=MESH
        )
    for i in range(1, C):
        pl.semaphore_signal(
            barrier, inc=1, device_id={"pts": me, "cen": (cen + i) % C}, device_id_type=MESH
        )
    load_points.wait()
    pl.semaphore_wait(barrier, 2 + C)

    def rows_of(t, h):
        return pts_all.at[pl.ds(pl.multiple_of(t * T + h * half, half), half)]

    def from_left(d):
        return tile_at((pos + R - d) % R, core)

    def from_right(d):
        return tile_at((pos + d) % R, core)

    def ring_copy(way, d, h, t):
        return pltpu.make_async_remote_copy(
            src_ref=rows_of(t, h), dst_ref=rows_of(t, h), send_sem=send_sem,
            recv_sem=ring_sem.at[way, d, h],
            device_id={"pts": (right, left)[way], "cen": cen}, device_id_type=MESH,
        )

    def twin_copy(way, d, h, t):
        return pltpu.make_async_remote_copy(
            src_ref=rows_of(t, h), dst_ref=rows_of(t, h), send_sem=send_sem,
            recv_sem=twin_sem.at[way, d, h],
            device_id={"pts": twin, "cen": cen}, device_id_type=MESH,
        )

    for h in range(2):
        ring_copy(0, 1, h, me).start()
        ring_copy(1, 1, 1 - h, me).start()
    for h in range(2):
        twin_copy(0, 0, h, me).start()

    load_table.wait()

    def norms(r, carry):
        rows = pl.ds(pl.multiple_of(r * RB, RB), RB)
        block = table[rows, :].astype(jnp.float32)
        total = jnp.sum(block * block, axis=1, keepdims=True)
        half_norms[rows, :] = jnp.broadcast_to(0.5 * total, (RB, T))
        return carry

    lax.fori_loop(0, NB, norms, 0)

    def process(t):
        cols = pl.ds(pl.multiple_of(t * T, T), T)
        tile = pts_all[cols, :]

        def score(r, top):
            rows = pl.ds(pl.multiple_of(r * RB, RB), RB)
            u = lax.dot_general(
                table[rows, :], tile, (((1,), (1,)), ((), ())),
                preferred_element_type=jnp.float32,
            ) - half_norms[rows, :]
            scores[rows, :] = u
            return jnp.maximum(top, jnp.max(u.reshape(RB // 8, 8, T), axis=0))

        top = lax.fori_loop(
            0, NB, score, jnp.full((8, T), -jnp.inf, jnp.float32), unroll=True
        )
        peak = jnp.max(top, axis=0, keepdims=True)

        def weigh(r, total):
            rows = pl.ds(pl.multiple_of(r * RB, RB), RB)
            e = jnp.exp2((scores[rows, :] - peak) * (2.0 * inv_temp * log2e))
            shares[rows, cols] = e.astype(jnp.bfloat16)
            return total + jnp.sum(e.reshape(RB // 8, 8, T), axis=0)

        total = lax.fori_loop(0, NB, weigh, jnp.zeros((8, T), jnp.float32), unroll=True)
        scaled_peak = peak * (2.0 * inv_temp)
        peaks[t] = scaled_peak
        value = scaled_peak + jnp.log(jnp.sum(total, axis=0, keepdims=True))
        local_log[t] = value

        @pl.when(t == me)
        def _():
            all_local[mine] = value

        def tell(c, carry):
            @pl.when(c * G + t != mine)
            def _():
                pltpu.make_async_remote_copy(
                    src_ref=local_log.at[t], dst_ref=all_local.at[mine],
                    send_sem=stat_send, recv_sem=stat_recv,
                    device_id={"pts": t, "cen": c}, device_id_type=MESH,
                ).start()
            return carry

        lax.fori_loop(0, C, tell, 0)

    other = 1 - 2 * core

    def twin_ready(way, d, t):
        for h in range(2):
            twin_copy(way, d, h, t).wait_recv()

    process(me)

    def step(d, carry):
        a, b = from_left(d), from_right(d)

        def pass_on(h0, h1):
            for way, h, t in ((0, h0, a), (1, h1, b)):
                ring_copy(way, d, h, t).wait_recv()

                @pl.when((d + 1 < far) | (h == way))
                def _():
                    ring_copy(way, d + 1, h, t).start()

                twin_copy(way, d, h, t).start()

        pass_on(0, 1)
        la, lb = from_left(d - 1) + other, from_right(d - 1) + other

        def earlier(k, carry):
            @pl.when(k == 0)
            def _():
                twin_ready(0, d - 1, la)

            @pl.when(k == 1)
            def _():
                twin_ready(1, d - 1, lb)

            process(la * (1 - k) + lb * k)
            return carry

        lax.fori_loop(0, jnp.minimum(d, 2), earlier, 0)
        pass_on(1, 0)

        def now(k, carry):
            process(a * (1 - k) + b * k)
            return carry

        lax.fori_loop(0, 2, now, 0)
        return carry

    lax.fori_loop(1, far, step, 0)

    last = from_left(far)
    for way in range(2):
        ring_copy(way, far, way, last).wait_recv()
        twin_copy(way, far, way, last).start()
    twin_ready(0, far - 1, from_left(far - 1) + other)
    twin_ready(1, far - 1, from_right(far - 1) + other)

    def tail(k, carry):
        @pl.when(k == 3)
        def _():
            for way in range(2):
                twin_copy(way, far, way, last + other).wait_recv()

        t = tile_at((pos + jnp.where(k == 0, R - far + 1, jnp.where(k == 1, far - 1, far))) % R, core)
        process(t + jnp.where(k == 2, 0, other))
        return carry

    lax.fori_loop(0, 4, tail, 0)

    pltpu.make_async_copy(
        all_local.at[pl.ds(0, N - 1)], all_local.at[pl.ds(0, N - 1)], stat_recv
    ).wait()
    logs = all_local[...].reshape(N, T)
    crest = jnp.max(logs, axis=0, keepdims=True)
    log_norm = crest + jnp.log(jnp.sum(jnp.exp(logs - crest), axis=0, keepdims=True))
    every_norm[me] = log_norm
    norm_ref[...] = log_norm

    def publish(i, carry):
        peer = (me + i) % G
        pltpu.make_async_remote_copy(
            src_ref=every_norm.at[me], dst_ref=every_norm.at[me],
            send_sem=norm_send, recv_sem=norm_recv,
            device_id={"pts": peer, "cen": cen}, device_id_type=MESH,
        ).start()
        return carry

    lax.fori_loop(1, G, publish, 0)
    group = every_norm.at[pl.ds(0, G - 1)]
    pltpu.make_async_copy(group, group, norm_recv).wait()

    def scale(t, carry):
        cols = pl.ds(pl.multiple_of(t * T, T), T)
        factor = jnp.exp(peaks[t] - every_norm[t])
        factors[:, cols] = jnp.broadcast_to(factor, (8, T))
        column = jnp.broadcast_to(factor, (8, T)).T[:, :1]
        pts_scaled[cols, :] = (pts_all[cols, :].astype(jnp.float32) * column).astype(jnp.bfloat16)
        return carry

    lax.fori_loop(0, G, scale, 0, unroll=8)

    KC = min(16, G)

    def update(r, carry):
        rows = pl.ds(pl.multiple_of(r * RB, RB), RB)

        def chunk(j, sums):
            weighted, mass = sums
            base = pl.multiple_of(j * KC * T, KC * T)
            weighted += jnp.dot(
                shares[rows, pl.ds(base, KC * T)], pts_scaled[pl.ds(base, KC * T), :],
                preferred_element_type=jnp.float32,
            )
            for k in range(KC):
                cols = pl.ds(pl.multiple_of(base + k * T, T), T)
                part = shares[rows, cols].astype(jnp.float32) * factors[:1, cols]
                for g in range(T // 128):
                    mass += part[:, g * 128:(g + 1) * 128]
            return weighted, mass

        start = (jnp.zeros((RB, D), jnp.float32), jnp.zeros((RB, 128), jnp.float32))
        weighted, mass = lax.fori_loop(0, G // KC, chunk, start, unroll=True)
        total = prior_count + jnp.sum(mass, axis=1, keepdims=True)
        out_ref[rows, :] = (table[rows, :].astype(jnp.float32) + weighted) / total
        return carry

    lax.fori_loop(0, NB, update, 0, unroll=2 if NB % 2 == 0 else 1)

    sent = pts_all.at[pl.ds(0, (G - 1) * T)]
    pltpu.make_async_copy(sent, sent, send_sem).wait()
    pltpu.make_async_copy(
        all_local.at[pl.ds(0, N - 1)], all_local.at[pl.ds(0, N - 1)], stat_send
    ).wait()
    pltpu.make_async_copy(group, group, norm_send).wait()


def body(G, C, points, centroids):
    T, D = points.shape
    own = centroids.shape[0] // G
    far = G // 4
    updated, log_norm = pl.pallas_call(
        functools.partial(kernel, G, C),
        out_shape=(
            pltpu.VMEM((own, D), jnp.float32),
            jax.ShapeDtypeStruct((1, T), jnp.float32),
        ),
        in_specs=[pl.BlockSpec(memory_space=pl.ANY)] * 2,
        out_specs=(pl.BlockSpec(memory_space=pltpu.VMEM),) * 2,
        scratch_shapes=[
            pltpu.VMEM((G * T, D), jnp.bfloat16),
            pltpu.VMEM((G * T, D), jnp.bfloat16),
            pltpu.VMEM((own, D), jnp.bfloat16),
            pltpu.VMEM((own, T), jnp.float32),
            pltpu.VMEM((own, T), jnp.float32),
            pltpu.VMEM((own, G * T), jnp.bfloat16),
            pltpu.VMEM((G, 1, T), jnp.float32),
            pltpu.VMEM((G, 1, T), jnp.float32),
            pltpu.VMEM((G * C, 1, T), jnp.float32),
            pltpu.VMEM((G, 1, T), jnp.float32),
            pltpu.VMEM((8, G * T), jnp.float32),
            pltpu.SemaphoreType.DMA((2,)),
            pltpu.SemaphoreType.DMA,
            pltpu.SemaphoreType.DMA((2, far + 1, 2)),
            pltpu.SemaphoreType.DMA((2, far + 1, 2)),
            pltpu.SemaphoreType.DMA,
            pltpu.SemaphoreType.DMA,
            pltpu.SemaphoreType.DMA,
            pltpu.SemaphoreType.DMA,
        ],
        compiler_params=pltpu.CompilerParams(
            collective_id=0, has_side_effects=True, vmem_limit_bytes=60 * 1024 * 1024
        ),
    )(points, centroids)
    return updated, log_norm.reshape(T)


def solution(mesh):
    placed = (P("pts", None), P("cen", None))
    return jax.shard_map(
        functools.partial(body, mesh.shape["pts"], mesh.shape["cen"]),
        mesh=mesh,
        in_specs=placed,
        out_specs=(P(("cen", "pts"), None), P("pts")),
        check_vma=False,
    )
```

profile of v0, /device:TPU:0, one launch (start us, length us, event | category | flops | bytes accessed | tf_op | source)
XLA Modules:
  0.0 42.6 jit_solution(2871812952010513966)
XLA Ops:
  0.6 40.1 %shard_map.41 = (f32[2048,256]{1,0:T(8,128)S(1)}, f32[1,256]{1,0:T(1,128)}) custom-call(bf16[256,256]{1,0:T(8,128)(2,1)} %points_ref.1, bf16[32768,256]{1,0:T(8,128)(2,1)} %table_ref.1), custom_call_target="tpu_custom_call" | custom-call | tf_op jit(solution)/shard_map/pallas_call | solution.py:292
  40.7 0.0 copy-start
  40.7 1.3 %copy.6 = f32[2048,256]{1,0:T(8,128)} copy(f32[2048,256]{1,0:T(8,128)S(1)} %get-tuple-element.6) | data formatting | bytes 4194304
  42.1 0.0 copy-done
  42.1 0.6 %copy.7 = f32[256]{0:T(256)} copy(f32[256]{0:T(256)S(1)} %bitcast.1) | data formatting | bytes 2048
Async XLA Ops:
  40.7 1.3 %copy-start = (f32[1,256]{1,0:T(1,128)S(1)}, f32[1,256]{1,0:T(1,128)}, u32[]{:S(2)}) copy-start(f32[1,256]{1,0:T(1,128)} %get-tuple-element.5) | copy-start | bytes 3076
where the time goes:
time: 42.8 us; the launch traced here: 42.6 us
  Pallas kernels  40.1 us (94%)
  local copies, waits for them, and re-layouts  1.89 us (4%)
  between operations  0.65 us (2%)
    pallas_call x1, Pallas kernels, body(): pl.pallas_call(functools.partial(kernel, G, C), out_shape=(pltpu.VMEM((ow...  40.1 us
    unnamed x4, local copies, waits for them, and re-layouts  1.89 us

commit v1 on v0

--- a/solution.py
+++ b/solution.py
@@ -25,6 +25,7 @@
     R = G // 2
     far = R // 2
     half = T // 2
+    W = T // 128
     N = G * C
     RB = min(256, own)
     NB = own // RB
@@ -126,7 +127,9 @@
         def weigh(r, total):
             rows = pl.ds(pl.multiple_of(r * RB, RB), RB)
             e = jnp.exp2((scores[rows, :] - peak) * (2.0 * inv_temp * log2e))
-            shares[rows, cols] = e.astype(jnp.bfloat16)
+            packed = e.astype(jnp.bfloat16)
+            for g in range(W):
+                shares[t * W + g, rows, :] = packed[:, g * 128:(g + 1) * 128]
             return total + jnp.sum(e.reshape(RB // 8, 8, T), axis=0)
 
         total = lax.fori_loop(0, NB, weigh, jnp.zeros((8, T), jnp.float32), unroll=True)
@@ -250,27 +253,26 @@
 
     lax.fori_loop(0, G, scale, 0, unroll=8)
 
-    KC = min(16, G)
+    KC = min(16, G) * W
 
     def update(r, carry):
         rows = pl.ds(pl.multiple_of(r * RB, RB), RB)
 
         def chunk(j, sums):
             weighted, mass = sums
-            base = pl.multiple_of(j * KC * T, KC * T)
+            base = pl.multiple_of(j * KC * 128, KC * 128)
+            parts = [shares[j * KC + g, rows, :] for g in range(KC)]
             weighted += jnp.dot(
-                shares[rows, pl.ds(base, KC * T)], pts_scaled[pl.ds(base, KC * T), :],
+                jnp.concatenate(parts, axis=1), pts_scaled[pl.ds(base, KC * 128), :],
                 preferred_element_type=jnp.float32,
             )
-            for k in range(KC):
-                cols = pl.ds(pl.multiple_of(base + k * T, T), T)
-                part = shares[rows, cols].astype(jnp.float32) * factors[:1, cols]
-                for g in range(T // 128):
-                    mass += part[:, g * 128:(g + 1) * 128]
+            for g in range(KC):
+                cols = pl.ds(pl.multiple_of(base + g * 128, 128), 128)
+                mass += parts[g].astype(jnp.float32) * factors[:1, cols]
             return weighted, mass
 
         start = (jnp.zeros((RB, D), jnp.float32), jnp.zeros((RB, 128), jnp.float32))
-        weighted, mass = lax.fori_loop(0, G // KC, chunk, start, unroll=True)
+        weighted, mass = lax.fori_loop(0, G * W // KC, chunk, start, unroll=True)
         total = prior_count + jnp.sum(mass, axis=1, keepdims=True)
         out_ref[rows, :] = (table[rows, :].astype(jnp.float32) + weighted) / total
         return carry
@@ -303,7 +305,7 @@
             pltpu.VMEM((own, D), jnp.bfloat16),
             pltpu.VMEM((own, T), jnp.float32),
             pltpu.VMEM((own, T), jnp.float32),
-            pltpu.VMEM((own, G * T), jnp.bfloat16),
+            pltpu.VMEM((G * T // 128, own, 128), jnp.bfloat16),
             pltpu.VMEM((G, 1, T), jnp.float32),
             pltpu.VMEM((G, 1, T), jnp.float32),
             pltpu.VMEM((G * C, 1, T), jnp.float32),

time: 42.8 us -> 40.5 us (0.946)
  Pallas kernels: 40.1 us -> 37.8 us
    pallas_call x1, Pallas kernels: 40.1 us -> 37.8 us  [body(): pl.pallas_call(functools.partial(kernel, G, C), out_shape=(pltpu.VMEM((ow...]
where the time goes in v1:
time: 40.5 us; the launch traced here: 40.3 us
  Pallas kernels  37.8 us (93%)
  local copies, waits for them, and re-layouts  1.89 us (5%)
  between operations  0.65 us (2%)
    pallas_call x1, Pallas kernels, body(): pl.pallas_call(functools.partial(kernel, G, C), out_shape=(pltpu.VMEM((ow...  37.8 us
    unnamed x4, local copies, waits for them, and re-layouts  1.89 us

profile of v1, /device:TPU:0, one launch (start us, length us, event | category | flops | bytes accessed | tf_op | source)
XLA Modules:
  0.0 40.3 jit_solution(10484032271745628725)
XLA Ops:
  0.6 37.8 %shard_map.41 = (f32[2048,256]{1,0:T(8,128)S(1)}, f32[1,256]{1,0:T(1,128)}) custom-call(bf16[256,256]{1,0:T(8,128)(2,1)} %points_ref.1, bf16[32768,256]{1,0:T(8,128)(2,1)} %table_ref.1), custom_call_target="tpu_custom_call" | custom-call | tf_op jit(solution)/shard_map/pallas_call | solution.py:294
  38.4 0.0 copy-start
  38.4 1.3 %copy.6 = f32[2048,256]{1,0:T(8,128)} copy(f32[2048,256]{1,0:T(8,128)S(1)} %get-tuple-element.6) | data formatting | bytes 4194304
  39.7 0.0 copy-done
  39.7 0.6 %copy.7 = f32[256]{0:T(256)} copy(f32[256]{0:T(256)S(1)} %bitcast.1) | data formatting | bytes 2048
Async XLA Ops:
  38.4 1.3 %copy-start = (f32[1,256]{1,0:T(1,128)S(1)}, f32[1,256]{1,0:T(1,128)}, u32[]{:S(2)}) copy-start(f32[1,256]{1,0:T(1,128)} %get-tuple-element.5) | copy-start | bytes 3076

commit v2 on v0

v2 whole, which is shorter than its diff:
```python
import functools
import math

import jax
import jax.numpy as jnp
from jax import lax
from jax.experimental import pallas as pl
from jax.experimental.pallas import tpu as pltpu
from jax.sharding import PartitionSpec as P

inv_temp = 0.0625
prior_count = 1.0
log2e = math.log2(math.e)
MESH = pl.DeviceIdType.MESH
Q = 4


def kernel(
    G, C, L, points_ref, table_ref, out_ref, norm_ref,
    pts_all, pts_scaled, table, half_norms, scores, shares,
    tops, peaks, near, wide, factors,
    load_sem, send_sem, ring_sem, twin_sem, near_send, near_recv, wide_send, wide_recv,
):
    T, D = points_ref.shape
    own = table.shape[0]
    W = T // 128
    R = G // 2
    far = R // 2
    piece = T // Q
    H = G // L
    RB = min(256, own)
    NB = own // RB
    me = lax.axis_index("pts")
    cen = lax.axis_index("cen")
    core = me % 2
    chip = me // 2
    turn = chip % 2
    pos = (chip // 2) * (1 - turn) + (R - 1 - chip // 2) * turn
    other = 1 - 2 * core
    hi = me // L
    slot = (me % L) * C + cen

    def tile_at(p, c):
        s = p // far
        return ((1 - s) * 2 * p + s * (2 * (R - 1 - p) + 1)) * 2 + c

    twin = me + other
    right = tile_at((pos + 1) % R, core)
    left = tile_at((pos + R - 1) % R, core)

    my_points = pts_all.at[pl.ds(pl.multiple_of(me * T, T), T)]
    load_points = pltpu.make_async_copy(points_ref, my_points, load_sem.at[0])
    load_points.start()
    load_table = pltpu.make_async_copy(
        table_ref.at[pl.ds(pl.multiple_of(me * own, own), own)], table, load_sem.at[1]
    )
    load_table.start()

    barrier = pltpu.get_barrier_semaphore()

    for peer in (right, left, twin):
        pl.semaphore_signal(
            barrier, inc=1, device_id={"pts": peer, "cen": cen}, device_id_type=MESH
        )
    for i in range(1, C):
        pl.semaphore_signal(
            barrier, inc=1, device_id={"pts": me, "cen": (cen + i) % C}, device_id_type=MESH
        )
    load_points.wait()
    pl.semaphore_wait(barrier, 2 + C)

    def from_side(way, d):
        return tile_at((pos + R + (2 * way - 1) * d) % R, core)

    def rows_of(t, q):
        return pts_all.at[pl.ds(pl.multiple_of(t * T + q * piece, piece), piece)]

    def ring_copy(way, d, q, t):
        return pltpu.make_async_remote_copy(
            src_ref=rows_of(t, q), dst_ref=rows_of(t, q), send_sem=send_sem,
            recv_sem=ring_sem.at[way, d, q],
            device_id={"pts": (right, left)[way], "cen": cen}, device_id_type=MESH,
        )

    def twin_copy(way, d, q, t):
        return pltpu.make_async_remote_copy(
            src_ref=rows_of(t, q), dst_ref=rows_of(t, q), send_sem=send_sem,
            recv_sem=twin_sem.at[way, d, q],
            device_id={"pts": twin, "cen": cen}, device_id_type=MESH,
        )

    for i in range(Q):
        ring_copy(0, 1, i, me).start()
        ring_copy(1, 1, Q - 1 - i, me).start()
    for q in range(Q):
        twin_copy(0, 0, q, me).start()

    def pass_on(d, i):
        for way in range(2):
            q = i if way == 0 else Q - 1 - i
            t = from_side(way, d)
            ring_copy(way, d, q, t).wait_recv()

            @pl.when((d + 1 < far) | ((d + 1 == far) & (i < Q // 2)))
            def _():
                ring_copy(way, d + 1, q, t).start()

            twin_copy(way, d, q, t).start()

    load_table.wait()

    def norms(r, carry):
        rows = pl.ds(pl.multiple_of(r * RB, RB), RB)
        block = table[rows, :].astype(jnp.float32)
        total = jnp.sum(block * block, axis=1, keepdims=True)
        half_norms[rows, :] = jnp.broadcast_to(0.5 * total, (RB, 128))
        return carry

    lax.fori_loop(0, NB, norms, 0, unroll=2 if NB % 2 == 0 else 1)

    lowest = jnp.full((8, T), -jnp.inf, jnp.float32)

    def score(tile, r, top):
        rows = slice(r * RB, (r + 1) * RB)
        u = lax.dot_general(
            table[rows, :], tile, (((1,), (1,)), ((), ())),
            preferred_element_type=jnp.float32,
        ) - jnp.concatenate([half_norms[rows, :]] * W, axis=1)
        scores[rows, :] = u
        return jnp.maximum(top, jnp.max(u.reshape(RB // 8, 8, T), axis=0))

    def weigh(t, r, peak, total):
        rows = slice(r * RB, (r + 1) * RB)
        e = jnp.exp2((scores[rows, :] - peak) * (2.0 * inv_temp * log2e))
        packed = e.astype(jnp.bfloat16)
        for g in range(W):
            shares[t * W + g, rows, :] = packed[:, g * 128:(g + 1) * 128]
        return total + jnp.sum(e.reshape(RB // 8, 8, T), axis=0)

    def finish(t, peak, total):
        scaled = peak * (2.0 * inv_temp)
        peaks[pl.ds(t, 1), :] = scaled
        near[slot, pl.ds(t, 1), :] = scaled + jnp.log(jnp.sum(total, axis=0, keepdims=True))

    def points_of(t):
        return pts_all[pl.ds(pl.multiple_of(t * T, T), T), :]

    def first(t):
        tile = points_of(t)
        top = lowest
        for r in range(NB):
            top = score(tile, r, top)
        tops[...] = top

    def advance(before, t):
        peak = jnp.max(tops[...], axis=0, keepdims=True)
        tile = points_of(t)
        top, total = lowest, jnp.zeros((8, T), jnp.float32)
        for r in range(NB):
            total = weigh(before, r, peak, total)
            top = score(tile, r, top)
        tops[...] = top
        finish(before, peak, total)

    def last(t):
        peak = jnp.max(tops[...], axis=0, keepdims=True)
        total = jnp.zeros((8, T), jnp.float32)
        for r in range(NB):
            total = weigh(t, r, peak, total)
        finish(t, peak, total)

    first(me)
    for q in range(Q):
        twin_copy(0, 0, q, twin).wait_recv()
    advance(me, twin)
    for i in range(Q - 1):
        pass_on(1, i)

    def step(j, before):
        d, k = 1 + j // 4, j % 4

        @pl.when(k == 0)
        def _():
            pass_on(d, Q - 1)

        @pl.when((k > 0) & (d + 1 < far))
        def _():
            pass_on(d + 1, k - 1)

        @pl.when((k > 1) & (d + 1 == far))
        def _():
            pass_on(d + 1, k - 2)

        for way in range(2):
            @pl.when(k == 2 + way)
            def _():
                t = from_side(way, d) + other
                for q in range(Q):
                    twin_copy(way, d, q, t).wait_recv()

        side = k % 2
        t = from_side(0, d) * (1 - side) + from_side(1, d) * side
        t = t + jnp.where(k >= 2, other, 0)
        advance(before, t)
        return t

    before = lax.fori_loop(0, 4 * (far - 1), step, twin)
    end = from_side(0, far)
    advance(before, end)
    for i in range(Q // 2):
        twin_copy(0, far, i, end + other).wait_recv()
        twin_copy(1, far, Q - 1 - i, end + other).wait_recv()
    advance(end, end + other)
    last(end + other)

    def tell(i, carry):
        s = (slot + i) % (L * C)
        pltpu.make_async_remote_copy(
            src_ref=near.at[slot], dst_ref=near.at[slot],
            send_sem=near_send, recv_sem=near_recv,
            device_id={"pts": hi * L + s // C, "cen": s % C}, device_id_type=MESH,
        ).start()
        return carry

    lax.fori_loop(1, L * C, tell, 0)
    near_group = near.at[pl.ds(0, L * C - 1)]
    pltpu.make_async_copy(near_group, near_group, near_recv).wait()

    def merge(logs):
        crest = jnp.max(logs, axis=0)
        return crest + jnp.log(jnp.sum(jnp.exp(logs - crest[None]), axis=0))

    wide[hi] = merge(near[...])

    def spread(i, carry):
        h = (hi + i) % H
        pltpu.make_async_remote_copy(
            src_ref=wide.at[hi], dst_ref=wide.at[hi],
            send_sem=wide_send, recv_sem=wide_recv,
            device_id={"pts": h * L + me % L, "cen": cen}, device_id_type=MESH,
        ).start()
        return carry

    lax.fori_loop(1, H, spread, 0)
    wide_group = wide.at[pl.ds(0, H - 1)]
    pltpu.make_async_copy(wide_group, wide_group, wide_recv).wait()
    log_norm = merge(wide[...])
    factors[...] = log_norm
    norm_ref[...] = factors[pl.ds(me, 1), :]
    factors[...] = jnp.exp(peaks[...] - log_norm)

    def scale(j, carry):
        columns = factors[pl.ds(pl.multiple_of(j * 8, 8), 8), :].T
        for i in range(8):
            rows = pl.ds(pl.multiple_of((j * 8 + i) * T, T), T)
            pts_scaled[rows, :] = (
                pts_all[rows, :].astype(jnp.float32) * columns[:, i:i + 1]
            ).astype(jnp.bfloat16)
        return carry

    lax.fori_loop(0, G // 8, scale, 0)

    KC = min(16, G)

    def update(r, carry):
        rows = pl.ds(pl.multiple_of(r * RB, RB), RB)
        weighted = jnp.zeros((RB, D), jnp.float32)
        mass = jnp.zeros((RB, 128), jnp.float32)
        for j in range(G // KC):
            parts = [shares[j * KC * W + g, rows, :] for g in range(KC * W)]
            weighted += jnp.dot(
                jnp.concatenate(parts, axis=1), pts_scaled[j * KC * T:(j + 1) * KC * T, :],
                preferred_element_type=jnp.float32,
            )
            for g in range(KC * W):
                t, h = j * KC + g // W, g % W
                mass += parts[g].astype(jnp.float32) * factors[t:t + 1, h * 128:(h + 1) * 128]
        total = prior_count + jnp.sum(mass, axis=1, keepdims=True)
        out_ref[rows, :] = (table[rows, :].astype(jnp.float32) + weighted) / total
        return carry

    lax.fori_loop(0, NB, update, 0, unroll=2 if NB % 2 == 0 else 1)

    sent = pts_all.at[pl.ds(0, (G - 1) * T)]
    pltpu.make_async_copy(sent, sent, send_sem).wait()
    pltpu.make_async_copy(near_group, near_group, near_send).wait()
    pltpu.make_async_copy(wide_group, wide_group, wide_send).wait()


def body(G, C, points, centroids):
    T, D = points.shape
    own = centroids.shape[0] // G
    far = G // 4
    L = 1 << ((G.bit_length() - 1) // 2)
    H = G // L
    updated, log_norm = pl.pallas_call(
        functools.partial(kernel, G, C, L),
        out_shape=(
            pltpu.VMEM((own, D), jnp.float32),
            jax.ShapeDtypeStruct((1, T), jnp.float32),
        ),
        in_specs=[pl.BlockSpec(memory_space=pl.ANY)] * 2,
        out_specs=(pl.BlockSpec(memory_space=pltpu.VMEM),) * 2,
        scratch_shapes=[
            pltpu.VMEM((G * T, D), jnp.bfloat16),
            pltpu.VMEM((G * T, D), jnp.bfloat16),
            pltpu.VMEM((own, D), jnp.bfloat16),
            pltpu.VMEM((own, 128), jnp.float32),
            pltpu.VMEM((own, T), jnp.float32),
            pltpu.VMEM((G * T // 128, own, 128), jnp.bfloat16),
            pltpu.VMEM((8, T), jnp.float32),
            pltpu.VMEM((G, T), jnp.float32),
            pltpu.VMEM((L * C, G, T), jnp.float32),
            pltpu.VMEM((H, G, T), jnp.float32),
            pltpu.VMEM((G, T), jnp.float32),
            pltpu.SemaphoreType.DMA((2,)),
            pltpu.SemaphoreType.DMA,
            pltpu.SemaphoreType.DMA((2, far + 1, Q)),
            pltpu.SemaphoreType.DMA((2, far + 1, Q)),
            pltpu.SemaphoreType.DMA,
            pltpu.SemaphoreType.DMA,
            pltpu.SemaphoreType.DMA,
            pltpu.SemaphoreType.DMA,
        ],
        compiler_params=pltpu.CompilerParams(
            collective_id=0, has_side_effects=True, vmem_limit_bytes=60 * 1024 * 1024
        ),
    )(points, centroids)
    return updated, log_norm.reshape(T)


def solution(mesh):
    placed = (P("pts", None), P("cen", None))
    return jax.shard_map(
        functools.partial(body, mesh.shape["pts"], mesh.shape["cen"]),
        mesh=mesh,
        in_specs=placed,
        out_specs=(P(("cen", "pts"), None), P("pts")),
        check_vma=False,
    )
```

time: 42.8 us -> 38.7 us (0.904)
  Pallas kernels: 40.1 us -> 36 us
    pallas_call x1, Pallas kernels: 40.1 us -> 36 us  [body(): pl.pallas_call(functools.partial(kernel, G, C, L), out_shape=(pltpu.VMEM(...]
where the time goes in v2:
time: 38.7 us; the launch traced here: 38.5 us
  Pallas kernels  36 us (93%)
  local copies, waits for them, and re-layouts  1.89 us (5%)
  between operations  0.65 us (2%)
    pallas_call x1, Pallas kernels, body(): pl.pallas_call(functools.partial(kernel, G, C, L), out_shape=(pltpu.VMEM(...  36 us
    unnamed x4, local copies, waits for them, and re-layouts  1.89 us

profile of v2, /device:TPU:0, one launch (start us, length us, event | category | flops | bytes accessed | tf_op | source)
XLA Modules:
  0.0 38.5 jit_solution(10902614631068958960)
XLA Ops:
  0.6 36.0 %shard_map.41 = (f32[2048,256]{1,0:T(8,128)S(1)}, f32[1,256]{1,0:T(1,128)}) custom-call(bf16[256,256]{1,0:T(8,128)(2,1)} %points_ref.1, bf16[32768,256]{1,0:T(8,128)(2,1)} %table_ref.1), custom_call_target="tpu_custom_call" | custom-call | tf_op jit(solution)/shard_map/pallas_call | solution.py:296
  36.6 0.0 copy-start
  36.6 1.3 %copy.6 = f32[2048,256]{1,0:T(8,128)} copy(f32[2048,256]{1,0:T(8,128)S(1)} %get-tuple-element.6) | data formatting | bytes 4194304
  37.9 0.0 copy-done
  37.9 0.6 %copy.7 = f32[256]{0:T(256)} copy(f32[256]{0:T(256)S(1)} %bitcast.1) | data formatting | bytes 2048
Async XLA Ops:
  36.6 1.3 %copy-start = (f32[1,256]{1,0:T(1,128)S(1)}, f32[1,256]{1,0:T(1,128)}, u32[]{:S(2)}) copy-start(f32[1,256]{1,0:T(1,128)} %get-tuple-element.5) | copy-start | bytes 3076

commit v3 on v2

--- a/solution.py
+++ b/solution.py
@@ -13,16 +13,18 @@
 log2e = math.log2(math.e)
 MESH = pl.DeviceIdType.MESH
 Q = 4
+A = 3
 
 
 def kernel(
     G, C, L, points_ref, table_ref, out_ref, norm_ref,
-    pts_all, pts_scaled, table, half_norms, scores, shares,
-    tops, peaks, near, wide, factors,
+    pts_all, pts_scaled, tables, half_norms, scores, shares,
+    tops, peaks, extra, near, wide, factors,
     load_sem, send_sem, ring_sem, twin_sem, near_send, near_recv, wide_send, wide_recv,
 ):
     T, D = points_ref.shape
-    own = table.shape[0]
+    own = tables.shape[1]
+    table = tables.at[A]
     W = T // 128
     R = G // 2
     far = R // 2
@@ -48,13 +50,22 @@
     right = tile_at((pos + 1) % R, core)
     left = tile_at((pos + R - 1) % R, core)
 
+    def from_side(way, d):
+        return tile_at((pos + R + (2 * way - 1) * d) % R, core)
+
     my_points = pts_all.at[pl.ds(pl.multiple_of(me * T, T), T)]
     load_points = pltpu.make_async_copy(points_ref, my_points, load_sem.at[0])
     load_points.start()
-    load_table = pltpu.make_async_copy(
-        table_ref.at[pl.ds(pl.multiple_of(me * own, own), own)], table, load_sem.at[1]
-    )
-    load_table.start()
+    blocks = (from_side(0, far - 1), from_side(1, far - 1), from_side(0, far), me)
+    loads = [
+        pltpu.make_async_copy(
+            table_ref.at[pl.ds(pl.multiple_of(block * own, own), own)],
+            tables.at[j], load_sem.at[1 + j],
+        )
+        for j, block in enumerate(blocks)
+    ]
+    for load in loads:
+        load.start()
 
     barrier = pltpu.get_barrier_semaphore()
 
@@ -68,9 +79,6 @@
         )
     load_points.wait()
     pl.semaphore_wait(barrier, 2 + C)
-
-    def from_side(way, d):
-        return tile_at((pos + R + (2 * way - 1) * d) % R, core)
 
     def rows_of(t, q):
         return pts_all.at[pl.ds(pl.multiple_of(t * T + q * piece, piece), piece)]
@@ -107,111 +115,126 @@
 
             twin_copy(way, d, q, t).start()
 
-    load_table.wait()
-
-    def norms(r, carry):
-        rows = pl.ds(pl.multiple_of(r * RB, RB), RB)
-        block = table[rows, :].astype(jnp.float32)
-        total = jnp.sum(block * block, axis=1, keepdims=True)
-        half_norms[rows, :] = jnp.broadcast_to(0.5 * total, (RB, 128))
-        return carry
-
-    lax.fori_loop(0, NB, norms, 0, unroll=2 if NB % 2 == 0 else 1)
+    near[slot] = jnp.full((G, T), -1e30, jnp.float32)
+
+    def norms(j):
+        def some(r, carry):
+            rows = pl.ds(pl.multiple_of(r * RB, RB), RB)
+            block = tables[j, rows, :].astype(jnp.float32)
+            total = jnp.sum(block * block, axis=1, keepdims=True)
+            half_norms[j % 2, rows, :] = jnp.broadcast_to(0.5 * total, (RB, 128))
+            return carry
+
+        lax.fori_loop(0, NB, some, 0, unroll=2 if NB % 2 == 0 else 1)
 
     lowest = jnp.full((8, T), -jnp.inf, jnp.float32)
 
-    def score(tile, r, top):
+    def score(j, tile, r, top):
         rows = slice(r * RB, (r + 1) * RB)
         u = lax.dot_general(
-            table[rows, :], tile, (((1,), (1,)), ((), ())),
+            tables[j, rows, :], tile, (((1,), (1,)), ((), ())),
             preferred_element_type=jnp.float32,
-        ) - jnp.concatenate([half_norms[rows, :]] * W, axis=1)
+        ) - jnp.concatenate([half_norms[j % 2, rows, :]] * W, axis=1)
         scores[rows, :] = u
         return jnp.maximum(top, jnp.max(u.reshape(RB // 8, 8, T), axis=0))
 
     def weigh(t, r, peak, total):
         rows = slice(r * RB, (r + 1) * RB)
         e = jnp.exp2((scores[rows, :] - peak) * (2.0 * inv_temp * log2e))
-        packed = e.astype(jnp.bfloat16)
-        for g in range(W):
-            shares[t * W + g, rows, :] = packed[:, g * 128:(g + 1) * 128]
+        if t is not None:
+            packed = e.astype(jnp.bfloat16)
+            for g in range(W):
+                shares[t * W + g, rows, :] = packed[:, g * 128:(g + 1) * 128]
         return total + jnp.sum(e.reshape(RB // 8, 8, T), axis=0)
 
     def finish(t, peak, total):
         scaled = peak * (2.0 * inv_temp)
-        peaks[pl.ds(t, 1), :] = scaled
-        near[slot, pl.ds(t, 1), :] = scaled + jnp.log(jnp.sum(total, axis=0, keepdims=True))
+        if t is not None:
+            peaks[pl.ds(t, 1), :] = scaled
+        return scaled + jnp.log(jnp.sum(total, axis=0, keepdims=True))
 
     def points_of(t):
         return pts_all[pl.ds(pl.multiple_of(t * T, T), T), :]
 
-    def first(t):
+    def advance(before, j, t):
         tile = points_of(t)
-        top = lowest
-        for r in range(NB):
-            top = score(tile, r, top)
-        tops[...] = top
-
-    def advance(before, t):
         peak = jnp.max(tops[...], axis=0, keepdims=True)
-        tile = points_of(t)
         top, total = lowest, jnp.zeros((8, T), jnp.float32)
         for r in range(NB):
             total = weigh(before, r, peak, total)
-            top = score(tile, r, top)
+            top = score(j, tile, r, top)
         tops[...] = top
-        finish(before, peak, total)
-
-    def last(t):
-        peak = jnp.max(tops[...], axis=0, keepdims=True)
-        total = jnp.zeros((8, T), jnp.float32)
-        for r in range(NB):
-            total = weigh(t, r, peak, total)
-        finish(t, peak, total)
-
-    first(me)
+        return finish(before, peak, total)
+
+    def piece_on(m):
+        pass_on(1 + m // Q, m % Q)
+
+    loads[0].wait()
+    norms(0)
+    tile = points_of(me)
+    top = lowest
+    for r in range(NB):
+        top = score(0, tile, r, top)
+    tops[...] = top
     for q in range(Q):
         twin_copy(0, 0, q, twin).wait_recv()
-    advance(me, twin)
-    for i in range(Q - 1):
-        pass_on(1, i)
-
-    def step(j, before):
-        d, k = 1 + j // 4, j % 4
-
-        @pl.when(k == 0)
+    def borrow(j, carry):
+        @pl.when(j > 0)
         def _():
-            pass_on(d, Q - 1)
-
-        @pl.when((k > 0) & (d + 1 < far))
-        def _():
-            pass_on(d + 1, k - 1)
-
-        @pl.when((k > 1) & (d + 1 == far))
-        def _():
-            pass_on(d + 1, k - 2)
-
+            piece_on(2 * j - 1)
+
+        extra[0, pl.ds(j, 1), :] = advance(None, j, twin)
+        pltpu.make_async_copy(
+            table_ref.at[pl.ds(0, own)], tables.at[j + 1], load_sem.at[j + 2]
+        ).wait()
+        norms(j + 1)
+        piece_on(2 * j)
+        extra[1, pl.ds(j, 1), :] = advance(None, j + 1, me)
+        return carry
+
+    lax.fori_loop(0, A, borrow, 0)
+    piece_on(2 * A - 1)
+    extra[0, A:A + 1, :] = advance(me, A, twin)
+
+    def tile_of(d, k):
+        side = k % 2
+        t = from_side(0, d) * (1 - side) + from_side(1, d) * side
+        return t + jnp.where(k >= 2, other, 0)
+
+    def arrived(d, k, t):
         for way in range(2):
             @pl.when(k == 2 + way)
             def _():
-                t = from_side(way, d) + other
                 for q in range(Q):
                     twin_copy(way, d, q, t).wait_recv()
 
-        side = k % 2
-        t = from_side(0, d) * (1 - side) + from_side(1, d) * side
-        t = t + jnp.where(k >= 2, other, 0)
-        advance(before, t)
+    def step(j, before):
+        d, k = 1 + j // 4, j % 4
+        t = tile_of(d, k)
+        piece_on(j + 2 * A)
+        arrived(d, k, t)
+        value = advance(before, A, t)
+
+        @pl.when(j == 0)
+        def _():
+            extra[1, A:A + 1, :] = value
+
+        @pl.when(j > 0)
+        def _():
+            near[slot, pl.ds(before, 1), :] = value
+
         return t
 
-    before = lax.fori_loop(0, 4 * (far - 1), step, twin)
-    end = from_side(0, far)
-    advance(before, end)
-    for i in range(Q // 2):
-        twin_copy(0, far, i, end + other).wait_recv()
-        twin_copy(1, far, Q - 1 - i, end + other).wait_recv()
-    advance(end, end + other)
-    last(end + other)
+    before = lax.fori_loop(0, 4 * (far - 2), step, twin)
+    t = tile_of(far - 1, 0)
+    near[slot, pl.ds(before, 1), :] = advance(before, A, t)
+    for i, home in enumerate((me, twin)):
+        parts = extra[i]
+        crest = jnp.max(parts, axis=0, keepdims=True)
+        near[slot, pl.ds(home, 1), :] = crest + jnp.log(
+            jnp.sum(jnp.exp(parts - crest), axis=0, keepdims=True)
+        )
+    before = t
 
     def tell(i, carry):
         s = (slot + i) % (L * C)
@@ -223,6 +246,16 @@
         return carry
 
     lax.fori_loop(1, L * C, tell, 0)
+    def distant(k, before):
+        t = tile_of(far - 1, k)
+        arrived(far - 1, k, t)
+        advance(before, A, t)
+        return t
+
+    before = lax.fori_loop(1, 4, distant, before)
+    end = from_side(0, far)
+    advance(before, A, end)
+
     near_group = near.at[pl.ds(0, L * C - 1)]
     pltpu.make_async_copy(near_group, near_group, near_recv).wait()
 
@@ -242,6 +275,15 @@
         return carry
 
     lax.fori_loop(1, H, spread, 0)
+    for i in range(Q // 2):
+        twin_copy(0, far, i, end + other).wait_recv()
+        twin_copy(1, far, Q - 1 - i, end + other).wait_recv()
+    advance(end, A, end + other)
+    peak = jnp.max(tops[...], axis=0, keepdims=True)
+    for r in range(NB):
+        weigh(end + other, r, peak, jnp.zeros((8, T), jnp.float32))
+    peaks[pl.ds(end + other, 1), :] = peak * (2.0 * inv_temp)
+
     wide_group = wide.at[pl.ds(0, H - 1)]
     pltpu.make_async_copy(wide_group, wide_group, wide_recv).wait()
     log_norm = merge(wide[...])
@@ -304,16 +346,17 @@
         scratch_shapes=[
             pltpu.VMEM((G * T, D), jnp.bfloat16),
             pltpu.VMEM((G * T, D), jnp.bfloat16),
-            pltpu.VMEM((own, D), jnp.bfloat16),
-            pltpu.VMEM((own, 128), jnp.float32),
+            pltpu.VMEM((A + 1, own, D), jnp.bfloat16),
+            pltpu.VMEM((2, own, 128), jnp.float32),
             pltpu.VMEM((own, T), jnp.float32),
             pltpu.VMEM((G * T // 128, own, 128), jnp.bfloat16),
             pltpu.VMEM((8, T), jnp.float32),
             pltpu.VMEM((G, T), jnp.float32),
+            pltpu.VMEM((2, A + 1, T), jnp.float32),
             pltpu.VMEM((L * C, G, T), jnp.float32),
             pltpu.VMEM((H, G, T), jnp.float32),
             pltpu.VMEM((G, T), jnp.float32),
-            pltpu.SemaphoreType.DMA((2,)),
+            pltpu.SemaphoreType.DMA((A + 2,)),
             pltpu.SemaphoreType.DMA,
             pltpu.SemaphoreType.DMA((2, far + 1, Q)),
             pltpu.SemaphoreType.DMA((2, far + 1, Q)),

time: 38.7 us -> 37.7 us (0.974)
  Pallas kernels: 36 us -> 35 us
    pallas_call x1, Pallas kernels: 36 us -> 35 us  [body(): pl.pallas_call(functools.partial(kernel, G, C, L), out_shape=(pltpu.VMEM(...]
where the time goes in v3:
time: 37.7 us; the launch traced here: 37.5 us
  Pallas kernels  35 us (93%)
  local copies, waits for them, and re-layouts  1.89 us (5%)
  between operations  0.65 us (2%)
    pallas_call x1, Pallas kernels, body(): pl.pallas_call(functools.partial(kernel, G, C, L), out_shape=(pltpu.VMEM(...  35 us
    unnamed x4, local copies, waits for them, and re-layouts  1.89 us

profile of v3, /device:TPU:0, one launch (start us, length us, event | category | flops | bytes accessed | tf_op | source)
XLA Modules:
  0.0 37.5 jit_solution(15375527774397444423)
XLA Ops:
  0.6 35.0 %shard_map.41 = (f32[2048,256]{1,0:T(8,128)S(1)}, f32[1,256]{1,0:T(1,128)}) custom-call(bf16[256,256]{1,0:T(8,128)(2,1)} %points_ref.1, bf16[32768,256]{1,0:T(8,128)(2,1)} %table_ref.1), custom_call_target="tpu_custom_call" | custom-call | tf_op jit(solution)/shard_map/pallas_call | solution.py:338
  35.6 0.0 copy-start
  35.6 1.3 %copy.6 = f32[2048,256]{1,0:T(8,128)} copy(f32[2048,256]{1,0:T(8,128)S(1)} %get-tuple-element.6) | data formatting | bytes 4194304
  36.9 0.0 copy-done
  36.9 0.6 %copy.7 = f32[256]{0:T(256)} copy(f32[256]{0:T(256)S(1)} %bitcast.1) | data formatting | bytes 2048
Async XLA Ops:
  35.6 1.3 %copy-start = (f32[1,256]{1,0:T(1,128)S(1)}, f32[1,256]{1,0:T(1,128)}, u32[]{:S(2)}) copy-start(f32[1,256]{1,0:T(1,128)} %get-tuple-element.5) | copy-start | bytes 3076

commit v4 on v3

--- a/solution.py
+++ b/solution.py
@@ -117,24 +117,18 @@
 
     near[slot] = jnp.full((G, T), -1e30, jnp.float32)
 
-    def norms(j):
-        def some(r, carry):
-            rows = pl.ds(pl.multiple_of(r * RB, RB), RB)
-            block = tables[j, rows, :].astype(jnp.float32)
-            total = jnp.sum(block * block, axis=1, keepdims=True)
-            half_norms[j % 2, rows, :] = jnp.broadcast_to(0.5 * total, (RB, 128))
-            return carry
-
-        lax.fori_loop(0, NB, some, 0, unroll=2 if NB % 2 == 0 else 1)
-
     lowest = jnp.full((8, T), -jnp.inf, jnp.float32)
 
-    def score(j, tile, r, top):
+    def score(j, tile, r, top, fresh):
         rows = slice(r * RB, (r + 1) * RB)
+        block = tables[j, rows, :]
+        if fresh:
+            wide_block = block.astype(jnp.float32)
+            total = jnp.sum(wide_block * wide_block, axis=1, keepdims=True)
+            half_norms[rows, :] = jnp.broadcast_to(0.5 * total, (RB, 128))
         u = lax.dot_general(
-            tables[j, rows, :], tile, (((1,), (1,)), ((), ())),
-            preferred_element_type=jnp.float32,
-        ) - jnp.concatenate([half_norms[j % 2, rows, :]] * W, axis=1)
+            block, tile, (((1,), (1,)), ((), ())), preferred_element_type=jnp.float32
+        ) - jnp.concatenate([half_norms[rows, :]] * W, axis=1)
         scores[rows, :] = u
         return jnp.maximum(top, jnp.max(u.reshape(RB // 8, 8, T), axis=0))
 
@@ -156,45 +150,50 @@
     def points_of(t):
         return pts_all[pl.ds(pl.multiple_of(t * T, T), T), :]
 
-    def advance(before, j, t):
-        tile = points_of(t)
-        peak = jnp.max(tops[...], axis=0, keepdims=True)
-        top, total = lowest, jnp.zeros((8, T), jnp.float32)
-        for r in range(NB):
-            total = weigh(before, r, peak, total)
-            top = score(j, tile, r, top)
+    def advance(before, *then):
+        top, values = tops[...], []
+        for j, t, fresh in then:
+            tile = points_of(t)
+            peak = jnp.max(top, axis=0, keepdims=True)
+            top, total = lowest, jnp.zeros((8, T), jnp.float32)
+            for r in range(NB):
+                total = weigh(before, r, peak, total)
+                top = score(j, tile, r, top, fresh)
+            values.append(finish(before, peak, total))
+            before = None if before is None else t
         tops[...] = top
-        return finish(before, peak, total)
+        return values
 
     def piece_on(m):
         pass_on(1 + m // Q, m % Q)
 
     loads[0].wait()
-    norms(0)
     tile = points_of(me)
     top = lowest
     for r in range(NB):
-        top = score(0, tile, r, top)
+        top = score(0, tile, r, top, True)
     tops[...] = top
     for q in range(Q):
         twin_copy(0, 0, q, twin).wait_recv()
+
     def borrow(j, carry):
+        @pl.when(j > 1)
+        def _():
+            piece_on(2 * j - 3)
+
         @pl.when(j > 0)
         def _():
-            piece_on(2 * j - 1)
-
-        extra[0, pl.ds(j, 1), :] = advance(None, j, twin)
+            piece_on(2 * j - 2)
+
         pltpu.make_async_copy(
             table_ref.at[pl.ds(0, own)], tables.at[j + 1], load_sem.at[j + 2]
         ).wait()
-        norms(j + 1)
-        piece_on(2 * j)
-        extra[1, pl.ds(j, 1), :] = advance(None, j + 1, me)
+        mine, twins = advance(None, (j, twin, False), (j + 1, me, True))
+        extra[0, pl.ds(j, 1), :] = mine
+        extra[1, pl.ds(j, 1), :] = twins
         return carry
 
     lax.fori_loop(0, A, borrow, 0)
-    piece_on(2 * A - 1)
-    extra[0, A:A + 1, :] = advance(me, A, twin)
 
     def tile_of(d, k):
         side = k % 2
@@ -208,34 +207,40 @@
                 for q in range(Q):
                     twin_copy(way, d, q, t).wait_recv()
 
-    def step(j, before):
-        d, k = 1 + j // 4, j % 4
-        t = tile_of(d, k)
-        piece_on(j + 2 * A)
-        arrived(d, k, t)
-        value = advance(before, A, t)
-
-        @pl.when(j == 0)
-        def _():
-            extra[1, A:A + 1, :] = value
-
-        @pl.when(j > 0)
-        def _():
-            near[slot, pl.ds(before, 1), :] = value
-
-        return t
-
-    before = lax.fori_loop(0, 4 * (far - 2), step, twin)
-    t = tile_of(far - 1, 0)
-    near[slot, pl.ds(before, 1), :] = advance(before, A, t)
+    def step(p, before):
+        piece_on(2 * p + 2 * A - 3)
+        piece_on(2 * p + 2 * A - 2)
+        j = 2 * p - 1
+        d0, k0, d1, k1 = 1 + j // 4, (j + 4) % 4, 1 + (j + 1) // 4, (j + 1) % 4
+        t0 = jnp.where(p == 0, twin, tile_of(d0, k0))
+        t1 = tile_of(d1, k1)
+
+        @pl.when(p > 0)
+        def _():
+            arrived(d0, k0, t0)
+
+        arrived(d1, k1, t1)
+        first, second = advance(before, (A, t0, False), (A, t1, False))
+
+        @pl.when(p == 0)
+        def _():
+            extra[0, A:A + 1, :] = first
+            extra[1, A:A + 1, :] = second
+
+        @pl.when(p > 0)
+        def _():
+            near[slot, pl.ds(before, 1), :] = first
+            near[slot, pl.ds(t0, 1), :] = second
+
+        return t1
+
+    before = lax.fori_loop(0, 2 * far - 3, step, me)
     for i, home in enumerate((me, twin)):
         parts = extra[i]
         crest = jnp.max(parts, axis=0, keepdims=True)
         near[slot, pl.ds(home, 1), :] = crest + jnp.log(
             jnp.sum(jnp.exp(parts - crest), axis=0, keepdims=True)
         )
-    before = t
-
     def tell(i, carry):
         s = (slot + i) % (L * C)
         pltpu.make_async_remote_copy(
@@ -246,15 +251,14 @@
         return carry
 
     lax.fori_loop(1, L * C, tell, 0)
-    def distant(k, before):
-        t = tile_of(far - 1, k)
-        arrived(far - 1, k, t)
-        advance(before, A, t)
-        return t
-
-    before = lax.fori_loop(1, 4, distant, before)
+    piece_on(Q * (far - 1) + 1)
+    for k in (1, 2):
+        arrived(far - 1, k, tile_of(far - 1, k))
+    second, third, fourth = (tile_of(far - 1, k) for k in (1, 2, 3))
+    advance(before, (A, second, False), (A, third, False))
     end = from_side(0, far)
-    advance(before, A, end)
+    arrived(far - 1, 3, fourth)
+    advance(third, (A, fourth, False), (A, end, False))
 
     near_group = near.at[pl.ds(0, L * C - 1)]
     pltpu.make_async_copy(near_group, near_group, near_recv).wait()
@@ -278,7 +282,7 @@
     for i in range(Q // 2):
         twin_copy(0, far, i, end + other).wait_recv()
         twin_copy(1, far, Q - 1 - i, end + other).wait_recv()
-    advance(end, A, end + other)
+    advance(end, (A, end + other, False))
     peak = jnp.max(tops[...], axis=0, keepdims=True)
     for r in range(NB):
         weigh(end + other, r, peak, jnp.zeros((8, T), jnp.float32))
@@ -347,7 +351,7 @@
             pltpu.VMEM((G * T, D), jnp.bfloat16),
             pltpu.VMEM((G * T, D), jnp.bfloat16),
             pltpu.VMEM((A + 1, own, D), jnp.bfloat16),
-            pltpu.VMEM((2, own, 128), jnp.float32),
+            pltpu.VMEM((own, 128), jnp.float32),
             pltpu.VMEM((own, T), jnp.float32),
             pltpu.VMEM((G * T // 128, own, 128), jnp.bfloat16),
             pltpu.VMEM((8, T), jnp.float32),

time: 37.7 us -> 36.6 us (0.971)
  Pallas kernels: 35 us -> 33.9 us
    pallas_call x1, Pallas kernels: 35 us -> 33.9 us  [body(): pl.pallas_call(functools.partial(kernel, G, C, L), out_shape=(pltpu.VMEM(...]
where the time goes in v4:
time: 36.6 us; the launch traced here: 36.4 us
  Pallas kernels  33.9 us (93%)
  local copies, waits for them, and re-layouts  1.89 us (5%)
  between operations  0.65 us (2%)
    pallas_call x1, Pallas kernels, body(): pl.pallas_call(functools.partial(kernel, G, C, L), out_shape=(pltpu.VMEM(...  33.9 us
    unnamed x4, local copies, waits for them, and re-layouts  1.89 us

profile of v4, /device:TPU:0, one launch (start us, length us, event | category | flops | bytes accessed | tf_op | source)
XLA Modules:
  0.0 36.4 jit_solution(11878703755137234471)
XLA Ops:
  0.6 33.9 %shard_map.41 = (f32[2048,256]{1,0:T(8,128)S(1)}, f32[1,256]{1,0:T(1,128)}) custom-call(bf16[256,256]{1,0:T(8,128)(2,1)} %points_ref.1, bf16[32768,256]{1,0:T(8,128)(2,1)} %table_ref.1), custom_call_target="tpu_custom_call" | custom-call | tf_op jit(solution)/shard_map/pallas_call | solution.py:342
  34.6 0.0 copy-start
  34.6 1.3 %copy.6 = f32[2048,256]{1,0:T(8,128)} copy(f32[2048,256]{1,0:T(8,128)S(1)} %get-tuple-element.6) | data formatting | bytes 4194304
  35.9 0.0 copy-done
  35.9 0.6 %copy.7 = f32[256]{0:T(256)} copy(f32[256]{0:T(256)S(1)} %bitcast.1) | data formatting | bytes 2048
Async XLA Ops:
  34.6 1.3 %copy-start = (f32[1,256]{1,0:T(1,128)S(1)}, f32[1,256]{1,0:T(1,128)}, u32[]{:S(2)}) copy-start(f32[1,256]{1,0:T(1,128)} %get-tuple-element.5) | copy-start | bytes 3076

commit v5 on v4

--- a/solution.py
+++ b/solution.py
@@ -12,7 +12,7 @@
 prior_count = 1.0
 log2e = math.log2(math.e)
 MESH = pl.DeviceIdType.MESH
-Q = 4
+Q = 2
 A = 3
 
 
@@ -29,9 +29,12 @@
     R = G // 2
     far = R // 2
     piece = T // Q
+    shift = Q.bit_length() - 1
     H = G // L
     RB = min(256, own)
     NB = own // RB
+    RS = min(1024, own)
+    NS = own // RS
     me = lax.axis_index("pts")
     cen = lax.axis_index("cen")
     core = me % 2
@@ -43,15 +46,17 @@
     slot = (me % L) * C + cen
 
     def tile_at(p, c):
-        s = p // far
-        return ((1 - s) * 2 * p + s * (2 * (R - 1 - p) + 1)) * 2 + c
+        return jnp.where(p < far, 2 * p, 2 * (R - 1 - p) + 1) * 2 + c
 
     twin = me + other
     right = tile_at((pos + 1) % R, core)
     left = tile_at((pos + R - 1) % R, core)
 
+    def around(p):
+        return p & (R - 1) if R & (R - 1) == 0 else lax.rem(p, R)
+
     def from_side(way, d):
-        return tile_at((pos + R + (2 * way - 1) * d) % R, core)
+        return tile_at(around(pos + R + (2 * way - 1) * d), core)
 
     my_points = pts_all.at[pl.ds(pl.multiple_of(me * T, T), T)]
     load_points = pltpu.make_async_copy(points_ref, my_points, load_sem.at[0])
@@ -74,11 +79,12 @@
             barrier, inc=1, device_id={"pts": peer, "cen": cen}, device_id_type=MESH
         )
     for i in range(1, C):
-        pl.semaphore_signal(
-            barrier, inc=1, device_id={"pts": me, "cen": (cen + i) % C}, device_id_type=MESH
-        )
+        for peer in (me, twin):
+            pl.semaphore_signal(
+                barrier, inc=1, device_id={"pts": peer, "cen": (cen + i) % C}, device_id_type=MESH
+            )
     load_points.wait()
-    pl.semaphore_wait(barrier, 2 + C)
+    pl.semaphore_wait(barrier, 1 + 2 * C)
 
     def rows_of(t, q):
         return pts_all.at[pl.ds(pl.multiple_of(t * T + q * piece, piece), piece)]
@@ -120,26 +126,26 @@
     lowest = jnp.full((8, T), -jnp.inf, jnp.float32)
 
     def score(j, tile, r, top, fresh):
-        rows = slice(r * RB, (r + 1) * RB)
+        rows = slice(r * RS, (r + 1) * RS)
         block = tables[j, rows, :]
         if fresh:
             wide_block = block.astype(jnp.float32)
             total = jnp.sum(wide_block * wide_block, axis=1, keepdims=True)
-            half_norms[rows, :] = jnp.broadcast_to(0.5 * total, (RB, 128))
+            half_norms[rows, :] = jnp.broadcast_to(0.5 * total, (RS, 128))
         u = lax.dot_general(
             block, tile, (((1,), (1,)), ((), ())), preferred_element_type=jnp.float32
         ) - jnp.concatenate([half_norms[rows, :]] * W, axis=1)
         scores[rows, :] = u
-        return jnp.maximum(top, jnp.max(u.reshape(RB // 8, 8, T), axis=0))
+        return jnp.maximum(top, jnp.max(u.reshape(RS // 8, 8, T), axis=0))
 
     def weigh(t, r, peak, total):
-        rows = slice(r * RB, (r + 1) * RB)
+        rows = slice(r * RS, (r + 1) * RS)
         e = jnp.exp2((scores[rows, :] - peak) * (2.0 * inv_temp * log2e))
         if t is not None:
             packed = e.astype(jnp.bfloat16)
             for g in range(W):
                 shares[t * W + g, rows, :] = packed[:, g * 128:(g + 1) * 128]
-        return total + jnp.sum(e.reshape(RB // 8, 8, T), axis=0)
+        return total + jnp.sum(e.reshape(RS // 8, 8, T), axis=0)
 
     def finish(t, peak, total):
         scaled = peak * (2.0 * inv_temp)
@@ -156,7 +162,7 @@
             tile = points_of(t)
             peak = jnp.max(top, axis=0, keepdims=True)
             top, total = lowest, jnp.zeros((8, T), jnp.float32)
-            for r in range(NB):
+            for r in range(NS):
                 total = weigh(before, r, peak, total)
                 top = score(j, tile, r, top, fresh)
             values.append(finish(before, peak, total))
@@ -165,12 +171,12 @@
         return values
 
     def piece_on(m):
-        pass_on(1 + m // Q, m % Q)
+        pass_on(1 + (m >> shift), m & (Q - 1))
 
     loads[0].wait()
     tile = points_of(me)
     top = lowest
-    for r in range(NB):
+    for r in range(NS):
         top = score(0, tile, r, top, True)
     tops[...] = top
     for q in range(Q):
@@ -179,11 +185,7 @@
     def borrow(j, carry):
         @pl.when(j > 1)
         def _():
-            piece_on(2 * j - 3)
-
-        @pl.when(j > 0)
-        def _():
-            piece_on(2 * j - 2)
+            piece_on(j - 2)
 
         pltpu.make_async_copy(
             table_ref.at[pl.ds(0, own)], tables.at[j + 1], load_sem.at[j + 2]
@@ -196,7 +198,7 @@
     lax.fori_loop(0, A, borrow, 0)
 
     def tile_of(d, k):
-        side = k % 2
+        side = k & 1
         t = from_side(0, d) * (1 - side) + from_side(1, d) * side
         return t + jnp.where(k >= 2, other, 0)
 
@@ -208,10 +210,9 @@
                     twin_copy(way, d, q, t).wait_recv()
 
     def step(p, before):
-        piece_on(2 * p + 2 * A - 3)
-        piece_on(2 * p + 2 * A - 2)
+        piece_on(p + A - 2)
         j = 2 * p - 1
-        d0, k0, d1, k1 = 1 + j // 4, (j + 4) % 4, 1 + (j + 1) // 4, (j + 1) % 4
+        d0, k0, d1, k1 = 1 + (j >> 2), j & 3, 1 + ((j + 1) >> 2), (j + 1) & 3
         t0 = jnp.where(p == 0, twin, tile_of(d0, k0))
         t1 = tile_of(d1, k1)
 
@@ -251,7 +252,7 @@
         return carry
 
     lax.fori_loop(1, L * C, tell, 0)
-    piece_on(Q * (far - 1) + 1)
+    piece_on(Q * (far - 1))
     for k in (1, 2):
         arrived(far - 1, k, tile_of(far - 1, k))
     second, third, fourth = (tile_of(far - 1, k) for k in (1, 2, 3))
@@ -284,7 +285,7 @@
         twin_copy(1, far, Q - 1 - i, end + other).wait_recv()
     advance(end, (A, end + other, False))
     peak = jnp.max(tops[...], axis=0, keepdims=True)
-    for r in range(NB):
+    for r in range(NS):
         weigh(end + other, r, peak, jnp.zeros((8, T), jnp.float32))
     peaks[pl.ds(end + other, 1), :] = peak * (2.0 * inv_temp)
 

time: 36.6 us -> 35.9 us (0.981)
  Pallas kernels: 33.9 us -> 33.2 us
    pallas_call x1, Pallas kernels: 33.9 us -> 33.2 us  [body(): pl.pallas_call(functools.partial(kernel, G, C, L), out_shape=(pltpu.VMEM(...]
where the time goes in v5:
time: 35.9 us; the launch traced here: 35.8 us
  Pallas kernels  33.2 us (92%)
  local copies, waits for them, and re-layouts  1.89 us (5%)
  between operations  0.65 us (2%)
    pallas_call x1, Pallas kernels, body(): pl.pallas_call(functools.partial(kernel, G, C, L), out_shape=(pltpu.VMEM(...  33.2 us
    unnamed x4, local copies, waits for them, and re-layouts  1.89 us

profile of v5, /device:TPU:0, one launch (start us, length us, event | category | flops | bytes accessed | tf_op | source)
XLA Modules:
  0.0 35.8 jit_solution(1169609709860397541)
XLA Ops:
  0.6 33.2 %shard_map.41 = (f32[2048,256]{1,0:T(8,128)S(1)}, f32[1,256]{1,0:T(1,128)}) custom-call(bf16[256,256]{1,0:T(8,128)(2,1)} %points_ref.1, bf16[32768,256]{1,0:T(8,128)(2,1)} %table_ref.1), custom_call_target="tpu_custom_call" | custom-call | tf_op jit(solution)/shard_map/pallas_call | solution.py:343
  33.9 0.0 copy-start
  33.9 1.3 %copy.6 = f32[2048,256]{1,0:T(8,128)} copy(f32[2048,256]{1,0:T(8,128)S(1)} %get-tuple-element.6) | data formatting | bytes 4194304
  35.2 0.0 copy-done
  35.2 0.6 %copy.7 = f32[256]{0:T(256)} copy(f32[256]{0:T(256)S(1)} %bitcast.1) | data formatting | bytes 2048
Async XLA Ops:
  33.9 1.3 %copy-start = (f32[1,256]{1,0:T(1,128)S(1)}, f32[1,256]{1,0:T(1,128)}, u32[]{:S(2)}) copy-start(f32[1,256]{1,0:T(1,128)} %get-tuple-element.5) | copy-start | bytes 3076

commit v6 on v5

--- a/solution.py
+++ b/solution.py
@@ -17,22 +17,19 @@
 
 
 def kernel(
-    G, C, L, points_ref, table_ref, out_ref, norm_ref,
-    pts_all, pts_scaled, tables, half_norms, scores, shares,
-    tops, peaks, extra, near, wide, factors,
+    G, C, L, points_ref, table_ref, shares, pts_scaled, factors, norm_ref, tables,
+    pts_all, half_norms, scores,
+    tops, peaks, extra, near, wide,
     load_sem, send_sem, ring_sem, twin_sem, near_send, near_recv, wide_send, wide_recv,
 ):
     T, D = points_ref.shape
     own = tables.shape[1]
-    table = tables.at[A]
     W = T // 128
     R = G // 2
     far = R // 2
     piece = T // Q
     shift = Q.bit_length() - 1
     H = G // L
-    RB = min(256, own)
-    NB = own // RB
     RS = min(1024, own)
     NS = own // RS
     me = lax.axis_index("pts")
@@ -307,6 +304,23 @@
 
     lax.fori_loop(0, G // 8, scale, 0)
 
+    sent = pts_all.at[pl.ds(0, (G - 1) * T)]
+    pltpu.make_async_copy(sent, sent, send_sem).wait()
+    pltpu.make_async_copy(near_group, near_group, near_send).wait()
+    pltpu.make_async_copy(wide_group, wide_group, wide_send).wait()
+
+
+def closing(G, shares, pts_scaled, factors, row_ref, tables, out_ref, norm_ref, staged, row, out_sem, row_sem):
+    table = tables.at[A]
+    own, D = staged.shape
+    T = factors.shape[1]
+    W = T // 128
+    RB = min(256, own)
+    NB = own // RB
+    row[...] = row_ref[0, :]
+    give = pltpu.make_async_copy(row, norm_ref, row_sem)
+    give.start()
+
     KC = min(16, G)
 
     def update(r, carry):
@@ -323,15 +337,14 @@
                 t, h = j * KC + g // W, g % W
                 mass += parts[g].astype(jnp.float32) * factors[t:t + 1, h * 128:(h + 1) * 128]
         total = prior_count + jnp.sum(mass, axis=1, keepdims=True)
-        out_ref[rows, :] = (table[rows, :].astype(jnp.float32) + weighted) / total
+        staged[rows, :] = (table[rows, :].astype(jnp.float32) + weighted) / total
+        pltpu.make_async_copy(staged.at[rows], out_ref.at[rows], out_sem).start()
         return carry
 
     lax.fori_loop(0, NB, update, 0, unroll=2 if NB % 2 == 0 else 1)
 
-    sent = pts_all.at[pl.ds(0, (G - 1) * T)]
-    pltpu.make_async_copy(sent, sent, send_sem).wait()
-    pltpu.make_async_copy(near_group, near_group, near_send).wait()
-    pltpu.make_async_copy(wide_group, wide_group, wide_send).wait()
+    give.wait()
+    pltpu.make_async_copy(staged, out_ref, out_sem).wait()
 
 
 def body(G, C, points, centroids):
@@ -340,27 +353,28 @@
     far = G // 4
     L = 1 << ((G.bit_length() - 1) // 2)
     H = G // L
-    updated, log_norm = pl.pallas_call(
+    grant = (66_900_000 - 2 * G * T * (own + D) - 2 * (A + 1) * own * D - 4 * (G + 8) * T) // 1024 * 1024
+    vmem, anywhere = pl.BlockSpec(memory_space=pltpu.VMEM), pl.BlockSpec(memory_space=pl.ANY)
+    parts = pl.pallas_call(
         functools.partial(kernel, G, C, L),
         out_shape=(
-            pltpu.VMEM((own, D), jnp.float32),
-            jax.ShapeDtypeStruct((1, T), jnp.float32),
+            pltpu.VMEM((G * T // 128, own, 128), jnp.bfloat16),
+            pltpu.VMEM((G * T, D), jnp.bfloat16),
+            pltpu.VMEM((G, T), jnp.float32),
+            pltpu.VMEM((1, T), jnp.float32),
+            pltpu.VMEM((A + 1, own, D), jnp.bfloat16),
         ),
-        in_specs=[pl.BlockSpec(memory_space=pl.ANY)] * 2,
-        out_specs=(pl.BlockSpec(memory_space=pltpu.VMEM),) * 2,
+        in_specs=[anywhere] * 2,
+        out_specs=(vmem,) * 5,
         scratch_shapes=[
             pltpu.VMEM((G * T, D), jnp.bfloat16),
-            pltpu.VMEM((G * T, D), jnp.bfloat16),
-            pltpu.VMEM((A + 1, own, D), jnp.bfloat16),
             pltpu.VMEM((own, 128), jnp.float32),
             pltpu.VMEM((own, T), jnp.float32),
-            pltpu.VMEM((G * T // 128, own, 128), jnp.bfloat16),
             pltpu.VMEM((8, T), jnp.float32),
             pltpu.VMEM((G, T), jnp.float32),
             pltpu.VMEM((2, A + 1, T), jnp.float32),
             pltpu.VMEM((L * C, G, T), jnp.float32),
             pltpu.VMEM((H, G, T), jnp.float32),
-            pltpu.VMEM((G, T), jnp.float32),
             pltpu.SemaphoreType.DMA((A + 2,)),
             pltpu.SemaphoreType.DMA,
             pltpu.SemaphoreType.DMA((2, far + 1, Q)),
@@ -371,10 +385,25 @@
             pltpu.SemaphoreType.DMA,
         ],
         compiler_params=pltpu.CompilerParams(
-            collective_id=0, has_side_effects=True, vmem_limit_bytes=60 * 1024 * 1024
+            collective_id=0, has_side_effects=True, vmem_limit_bytes=grant
         ),
     )(points, centroids)
-    return updated, log_norm.reshape(T)
+    return pl.pallas_call(
+        functools.partial(closing, G),
+        out_shape=(
+            jax.ShapeDtypeStruct((own, D), jnp.float32),
+            jax.ShapeDtypeStruct((T,), jnp.float32),
+        ),
+        in_specs=[vmem] * 5,
+        out_specs=(anywhere, anywhere),
+        scratch_shapes=[
+            pltpu.VMEM((own, D), jnp.float32),
+            pltpu.VMEM((T,), jnp.float32),
+            pltpu.SemaphoreType.DMA,
+            pltpu.SemaphoreType.DMA,
+        ],
+        compiler_params=pltpu.CompilerParams(vmem_limit_bytes=16 * 1024 * 1024),
+    )(*parts)
 
 
 def solution(mesh):

time: 35.9 us -> 34.3 us (0.955)
  local copies, waits for them, and re-layouts: 1.89 us -> 0 us
    pallas_call x0 -> x1, Pallas kernels: none -> 6.18 us  [body(): pl.pallas_call(functools.partial(closing, G), out_shape=(jax.ShapeDtypeSt...]
    pallas_call x1, Pallas kernels: 33.2 us -> 27.3 us  [body(): pl.pallas_call(functools.partial(kernel, G, C, L), out_shape=(pltpu.VMEM(...]
    unnamed x4 -> x0, local copies, waits for them, and re-layouts: 1.89 us -> none
where the time goes in v6:
time: 34.3 us; the launch traced here: 34.1 us
  Pallas kernels  33.5 us (98%)
  between operations  0.64 us (2%)
    pallas_call x1, Pallas kernels, body(): pl.pallas_call(functools.partial(kernel, G, C, L), out_shape=(pltpu.VMEM(...  27.3 us
    pallas_call x1, Pallas kernels, body(): pl.pallas_call(functools.partial(closing, G), out_shape=(jax.ShapeDtypeSt...  6.18 us

profile of v6, /device:TPU:0, one launch (start us, length us, event | category | flops | bytes accessed | tf_op | source)
XLA Modules:
  0.0 34.1 jit_solution(2606515997396959786)
XLA Ops:
  0.6 27.3 %shard_map.41 = (bf16[32,2048,128]{2,1,0:T(8,128)(2,1)S(1)}, bf16[4096,256]{1,0:T(8,128)(2,1)S(1)}, f32[16,256]{1,0:T(8,128)S(1)}, f32[1,256]{1,0:T(1,128)S(1)}, bf16[4,2048,256]{2,1,0:T(8,128)(2,1)S(1)}) custom-call(bf16[256,256]{1,0:T(8,128)(2,1)} %points_ref.1, bf16[32768,256]{1,0:T(8,128)(2,1)} %table_ref.1), custom_call_target="tpu_custom_call" | custom-call | tf_op jit(solution)/shard_map/pallas_call | solution.py:358
  27.9 6.2 %shard_map.42 = (f32[2048,256]{1,0:T(8,128)}, f32[256]{0:T(256)}) custom-call(bf16[32,2048,128]{2,1,0:T(8,128)(2,1)S(1)} %get-tuple-element.7.shares, bf16[4096,256]{1,0:T(8,128)(2,1)S(1)} %get-tuple-element.8.pts_scaled, f32[16,256]{1,0:T(8,128)S(1)} %get-tuple-element.9.factors, f32[1,256]{1,0:T(1,128)S(1)} %get-tuple-element.10.row_ref, ...), custom_call_target="tpu_custom_call" | custom-call | tf_op jit(solution)/shard_map/pallas_call | solution.py:391

commit v7 on v6

--- a/solution.py
+++ b/solution.py
@@ -232,7 +232,15 @@
 
         return t1
 
-    before = lax.fori_loop(0, 2 * far - 3, step, me)
+    before = lax.fori_loop(0, 2 * far - 4, step, me)
+    t = tile_of(far - 2, 3)
+    arrived(far - 2, 3, t)
+    near[slot, pl.ds(before, 1), :] = advance(before, (A, t, False))[0]
+    peak = jnp.max(tops[...], axis=0, keepdims=True)
+    total = jnp.zeros((8, T), jnp.float32)
+    for r in range(NS):
+        total = weigh(t, r, peak, total)
+    near[slot, pl.ds(t, 1), :] = finish(t, peak, total)
     for i, home in enumerate((me, twin)):
         parts = extra[i]
         crest = jnp.max(parts, axis=0, keepdims=True)
@@ -249,7 +257,14 @@
         return carry
 
     lax.fori_loop(1, L * C, tell, 0)
+    piece_on(Q * (far - 1) - 1)
     piece_on(Q * (far - 1))
+    before = tile_of(far - 1, 0)
+    tile = points_of(before)
+    top = lowest
+    for r in range(NS):
+        top = score(A, tile, r, top, False)
+    tops[...] = top
     for k in (1, 2):
         arrived(far - 1, k, tile_of(far - 1, k))
     second, third, fourth = (tile_of(far - 1, k) for k in (1, 2, 3))
@@ -302,7 +317,7 @@
             ).astype(jnp.bfloat16)
         return carry
 
-    lax.fori_loop(0, G // 8, scale, 0)
+    lax.fori_loop(0, G // 8, scale, 0, unroll=G <= 16)
 
     sent = pts_all.at[pl.ds(0, (G - 1) * T)]
     pltpu.make_async_copy(sent, sent, send_sem).wait()

time: 34.3 us -> 34 us (level)
  no operation moved by 1% of the time
where the time goes in v7:
time: 34 us; the launch traced here: 33.8 us
  Pallas kernels  33.2 us (98%)
  between operations  0.64 us (2%)
    pallas_call x1, Pallas kernels, body(): pl.pallas_call(functools.partial(kernel, G, C, L), out_shape=(pltpu.VMEM(...  27 us
    pallas_call x1, Pallas kernels, body(): pl.pallas_call(functools.partial(closing, G), out_shape=(jax.ShapeDtypeSt...  6.19 us

profile of v7, /device:TPU:0, one launch (start us, length us, event | category | flops | bytes accessed | tf_op | source)
XLA Modules:
  0.0 33.8 jit_solution(6573538534661058561)
XLA Ops:
  0.6 27.0 %shard_map.41 = (bf16[32,2048,128]{2,1,0:T(8,128)(2,1)S(1)}, bf16[4096,256]{1,0:T(8,128)(2,1)S(1)}, f32[16,256]{1,0:T(8,128)S(1)}, f32[1,256]{1,0:T(1,128)S(1)}, bf16[4,2048,256]{2,1,0:T(8,128)(2,1)S(1)}) custom-call(bf16[256,256]{1,0:T(8,128)(2,1)} %points_ref.1, bf16[32768,256]{1,0:T(8,128)(2,1)} %table_ref.1), custom_call_target="tpu_custom_call" | custom-call | tf_op jit(solution)/shard_map/pallas_call | solution.py:373
  27.6 6.2 %shard_map.42 = (f32[2048,256]{1,0:T(8,128)}, f32[256]{0:T(256)}) custom-call(bf16[32,2048,128]{2,1,0:T(8,128)(2,1)S(1)} %get-tuple-element.7.shares, bf16[4096,256]{1,0:T(8,128)(2,1)S(1)} %get-tuple-element.8.pts_scaled, f32[16,256]{1,0:T(8,128)S(1)} %get-tuple-element.9.factors, f32[1,256]{1,0:T(1,128)S(1)} %get-tuple-element.10.row_ref, ...), custom_call_target="tpu_custom_call" | custom-call | tf_op jit(solution)/shard_map/pallas_call | solution.py:406
